TPU v7x, 32 devices: a whole 2x2x4 slice. The times are simulated.
32 devices in a mesh: grp: 4 (over z), slab: 8 (over y, x, core).
Axes of the slice: x: 2, y: 2, z: 4, core: 2. Of those that a mesh axis runs over, the one named last changes fastest.
Arguments:
- tensor: float32 [672, 64, 672], P('grp', 'slab'), may hold values from -20 to 20
- start_one: float32 [672, 96], replicated, may hold values from -6 to 6
- start_two: float32 [672, 96], replicated, may hold values from -6 to 6
Outputs:
- basis_one: float32 [672, 96], replicated
- basis_two: float32 [672, 96], replicated
- core: float32 [96, 64, 96], P('grp', 'slab')
All inputs are finite; a program needn't handle non-finite values.
Results may differ from a plain program's by a relative error of at most 0.0003.
Values sent between devices are 32-bit elements; how exact they have to be, the bound alone decides.
No kernel may reach another device: no remote copies, remote signals or barrier semaphores. Data moves between devices by JAX's collectives and lax.ppermute only.
A program may use at most 64 MiB of HBM per device.

v0:
```python
import jax
import jax.numpy as jnp
from jax import lax
from jax.sharding import PartitionSpec as P

ITERS = 2
HIGH = lax.Precision.HIGHEST


def orthonormal(widened):
    cross = jnp.dot(widened.T, widened, precision=HIGH)
    lower_small = jnp.linalg.cholesky(cross)
    return lax.linalg.triangular_solve(
        lower_small, widened, left_side=False, lower=True, transpose_a=True
    )


def iterate_basis(gram, start):
    current = start
    for _ in range(ITERS):
        current = orthonormal(jnp.dot(gram, current, precision=HIGH))
    return current


def local(tensor, start_one, start_two):
    block_gram = jnp.einsum("jmi,jmk->ik", tensor, tensor, precision=HIGH)
    gram_one = lax.psum(block_gram, ("grp", "slab"))
    basis_one = iterate_basis(gram_one, start_one)
    reduced = jnp.einsum("jmi,ia->jma", tensor, basis_one, precision=HIGH)
    regrouped = lax.all_to_all(reduced, "grp", split_axis=1, concat_axis=0, tiled=True)
    block_second = jnp.einsum("jma,kma->jk", regrouped, regrouped, precision=HIGH)
    gram_two = lax.psum(block_second, ("grp", "slab"))
    basis_two = iterate_basis(gram_two, start_two)
    core_block = jnp.einsum("jb,jma->bma", basis_two, regrouped, precision=HIGH)
    core = lax.all_to_all(core_block, "grp", split_axis=0, concat_axis=1, tiled=True)
    return (basis_one, basis_two, core)


def solution(mesh):
    in_specs = (P("grp", "slab", None), P(), P())
    out_specs = (P(), P(), P("grp", "slab", None))
    return jax.shard_map(local, mesh=mesh, in_specs=in_specs, out_specs=out_specs, check_vma=False)
```

profile of v0, /device:TPU:0, one launch (start us, length us, event | category | flops | bytes accessed | tf_op | source)
XLA Modules:
  0.0 439.0 jit_solution(15188821805483427743)
XLA Ops:
  7.2 18.1 %fusion.4 = f32[672,672]{1,0:T(8,128)} fusion(f32[168,8,672]{2,1,0:T(8,128)} %param.6), kind=kOutput, calls=%fused_computation.5 | convolution fusion | flops 7283146752 | bytes 5419008 | tf_op jit(solution)/shard_map/jmi,jmk->ik/dot_general | solution.py:26
  25.8 136.7 %all-reduce.3.cloned.1.call-done = f32[672,672]{1,0:T(8,128)} async-done(((f32[672,672]{1,0:T(8,128)}), f32[672,672]{1,0:T(8,128)}) %all-reduce.3.cloned.1.call-update) | async-done | bytes 1806352 | tf_op jit(solution)/shard_map/psum | solution.py:27
  162.4 3.7 fusion.29
  166.6 8.8 %cholesky.74 = f32[96,96]{1,0:T(8,128)S(1)} custom-call(f32[96,96]{1,0:T(8,128)S(1)} %fusion.26), custom_call_target="Cholesky" | custom-call | tf_op jit(solution)/shard_map/jit(cholesky)/cholesky | solution.py:12
  176.1 0.7 fusion.13
  176.7 7.4 %custom-call.8 = f32[1,96,96]{1,2,0:T(8,128)S(1)} custom-call(f32[1,96,96]{2,1,0:T(8,128)S(1)} %fusion.13), custom_call_target="InvertDiagBlocksLowerTriangular" | custom-call | tf_op jit(solution)/shard_map/triangular_solve/custom-call.0 | solution.py:13
  184.6 2.0 fusion.31
  187.0 8.8 %cholesky.85 = f32[96,96]{1,0:T(8,128)S(1)} custom-call(f32[96,96]{1,0:T(8,128)S(1)} %fusion.24), custom_call_target="Cholesky" | custom-call | tf_op jit(solution)/shard_map/jit(cholesky)/cholesky | solution.py:12
  196.5 0.7 fusion.14
  197.2 7.4 %custom-call.9 = f32[1,96,96]{1,2,0:T(8,128)S(1)} custom-call(f32[1,96,96]{2,1,0:T(8,128)S(1)} %fusion.14), custom_call_target="InvertDiagBlocksLowerTriangular" | custom-call | tf_op jit(solution)/shard_map/triangular_solve/custom-call.0 | solution.py:13
  205.0 17.6 %fusion.7 = f32[168,8,96]{2,0,1:T(8,128)S(1)} fusion(f32[168,8,672]{2,1,0:T(8,128)} %param.6, f32[96,672]{1,0:T(8,128)S(1)} %fusion.22), kind=kOutput, calls=%fused_computation.6 | convolution fusion | flops 1040449536 | bytes 4386816 | tf_op jit(solution)/shard_map/jmi,ia->jma/dot_general | solution.py:29
  222.7 19.8 %all_to_all.36 = f32[168,8,96]{2,0,1:T(8,128)S(1)} all-to-all(f32[168,8,96]{2,0,1:T(8,128)S(1)} %fusion.7), channel_id=1, replica_groups=mesh['grp'=4,'slab'=8] {'grp'}, dimensions={1} | all-to-all | bytes 1032192 | tf_op jit(solution)/shard_map/all_to_all | solution.py:30
  242.5 3.1 convolution_bitcast_fusion
  245.6 133.2 %all-reduce.5.cloned.1.call-done = f32[672,672]{1,0:T(8,128)} async-done(((f32[672,672]{1,0:T(8,128)}), f32[672,672]{1,0:T(8,128)}) %all-reduce.5.cloned.1.call-update) | async-done | bytes 1806352 | tf_op jit(solution)/shard_map/psum | solution.py:32
  378.8 3.7 fusion.33
  383.0 8.8 %cholesky.96 = f32[96,96]{1,0:T(8,128)S(1)} custom-call(f32[96,96]{1,0:T(8,128)S(1)} %fusion.21), custom_call_target="Cholesky" | custom-call | tf_op jit(solution)/shard_map/jit(cholesky)/cholesky | solution.py:12
  392.4 0.7 fusion.15
  393.1 7.4 %custom-call.10 = f32[1,96,96]{1,2,0:T(8,128)S(1)} custom-call(f32[1,96,96]{2,1,0:T(8,128)S(1)} %fusion.15), custom_call_target="InvertDiagBlocksLowerTriangular" | custom-call | tf_op jit(solution)/shard_map/triangular_solve/custom-call.0 | solution.py:13
  400.9 2.0 fusion.35
  403.4 8.9 %cholesky.107 = f32[96,96]{1,0:T(8,128)S(1)} custom-call(f32[96,96]{1,0:T(8,128)S(1)} %fusion.19), custom_call_target="Cholesky" | custom-call | tf_op jit(solution)/shard_map/jit(cholesky)/cholesky | solution.py:12
  413.0 0.7 fusion.16
  413.6 7.4 %custom-call.11 = f32[1,96,96]{1,2,0:T(8,128)S(1)} custom-call(f32[1,96,96]{2,1,0:T(8,128)S(1)} %fusion.16), custom_call_target="InvertDiagBlocksLowerTriangular" | custom-call | tf_op jit(solution)/shard_map/triangular_solve/custom-call.0 | solution.py:13
  422.0 9.2 %all_to_all.37 = f32[96,2,96]{2,1,0:T(2,128)S(1)} all-to-all(f32[96,2,96]{2,1,0:T(2,128)S(1)} %copy.38), channel_id=1, replica_groups=mesh['grp'=4,'slab'=8] {'grp'}, dimensions={0} | all-to-all | bytes 147456 | tf_op jit(solution)/shard_map/all_to_all | solution.py:35
  431.3 0.7 copy.39
  (41 shorter events, 7.5 us)
Async XLA Ops:
  7.2 155.3 %copy-start = (f32[672,96]{0,1:T(8,128)S(1)}, f32[672,96]{0,1:T(8,128)}, u32[]{:S(2)}) copy-start(f32[672,96]{0,1:T(8,128)} %param.7) | copy-start | bytes 774148
  7.2 155.2 %all-reduce.3.cloned.1.call-start = ((), (), s32[]{:S(2)}) async-start(), calls=%async_computation.2 | async-start | bytes 4128768 | tf_op jit(solution)/shard_map/psum | solution.py:27
  25.3 353.5 %all-reduce.5.cloned.1.call-start = ((), (), s32[]{:S(2)}) async-start(), calls=%async_computation.3 | async-start | bytes 4128768 | tf_op jit(solution)/shard_map/psum | solution.py:32
  162.4 22.1 %copy-start.1 = (f32[672,672]{1,0:T(8,128)S(1)}, f32[672,672]{1,0:T(8,128)}, u32[]{:S(2)}) copy-start(f32[672,672]{1,0:T(8,128)} %all-reduce.3.cloned.1.call-done) | copy-start | bytes 5419012
  205.0 17.7 %copy-start.3 = (f32[96,672]{1,0:T(8,128)}, f32[96,672]{1,0:T(8,128)S(1)}, u32[]{:S(2)}) copy-start(f32[96,672]{1,0:T(8,128)S(1)} %fusion.22) | copy-start | bytes 774148
  378.8 22.1 %copy-start.2 = (f32[672,672]{1,0:T(8,128)S(1)}, f32[672,672]{1,0:T(8,128)}, u32[]{:S(2)}) copy-start(f32[672,672]{1,0:T(8,128)} %all-reduce.5.cloned.1.call-done) | copy-start | bytes 5419012
  421.4 10.5 %copy-start.4 = (f32[96,672]{1,0:T(8,128)}, f32[96,672]{1,0:T(8,128)S(1)}, u32[]{:S(2)}) copy-start(f32[96,672]{1,0:T(8,128)S(1)} %fusion.17) | copy-start | bytes 774148
Sparse Core Ops, SparseCore 0:
  25.4 136.9 all-reduce.2
  245.7 133.0 all-reduce.4
where the time goes:
time: 445 us; the launch traced here: 439 us
  waiting for transfers between devices  270 us (61%)
  other arithmetic  70 us (16%)
  matrix products  53.9 us (12%)
  blocking collectives  29 us (7%)
  between operations  14.6 us (3%)
    psum x1, waiting for transfers between devices, local(): gram_one = lax.psum(block_gram, ('grp', 'slab'))  137 us
    psum x1, waiting for transfers between devices, local(): gram_two = lax.psum(block_second, ('grp', 'slab'))  133 us
    another operation x12, other arithmetic, orthonormal(): lower_small = jnp.linalg.cholesky(cross)  37.9 us
    another operation x8, other arithmetic, orthonormal(): lax.linalg.triangular_solve(lower_small, widened, left_side=False, lower=...  32 us
    all_to_all x1, blocking collectives, local(): lax.all_to_all(reduced, 'grp', split_axis=1, concat_axis=0, tiled=True)  19.8 us
    dot_general x1, matrix products, local(): block_gram = jnp.einsum('jmi,jmk->ik', tensor, tensor, precision=HIGH)  18.1 us
    dot_general x1, matrix products, local(): reduced = jnp.einsum('jmi,ia->jma', tensor, basis_one, precision=HIGH)  17.6 us
    dot_general x4, matrix products, iterate_basis(): current = orthonormal(jnp.dot(gram, current, precision=HIGH))  11.3 us
  transfers between devices with their start and end apart: 2, of which 2 were waited for; matrix products, arithmetic and copies ran while one was open for 0% of the time, Pallas kernels for 0%

commit v1 on v0

--- a/solution.py
+++ b/solution.py
@@ -24,7 +24,7 @@
 
 def local(tensor, start_one, start_two):
     block_gram = jnp.einsum("jmi,jmk->ik", tensor, tensor, precision=HIGH)
-    gram_one = lax.psum(block_gram, ("grp", "slab"))
+    gram_one = lax.psum(lax.psum(block_gram, "slab"), "grp")
     basis_one = iterate_basis(gram_one, start_one)
     reduced = jnp.einsum("jmi,ia->jma", tensor, basis_one, precision=HIGH)
     regrouped = lax.all_to_all(reduced, "grp", split_axis=1, concat_axis=0, tiled=True)

time: 445 us -> 460 us (1.034)
  waiting for transfers between devices: 270 us -> 284 us
    psum x1 -> x2, waiting for transfers between devices: 137 us -> 151 us  [local(): gram_one = lax.psum(lax.psum(block_gram, 'slab'), 'grp')]
  transfers between devices with their start and end apart: 2 -> 3, of which waited for: 2 -> 3; matrix products, arithmetic and copies ran while one was open for 0% -> 0% of each run, Pallas kernels for 0% -> 0%
where the time goes in v1:
time: 460 us; the launch traced here: 454 us
  waiting for transfers between devices  284 us (62%)
  other arithmetic  70 us (15%)
  matrix products  53.9 us (12%)
  blocking collectives  30.1 us (7%)
  between operations  14.3 us (3%)
    psum x2, waiting for transfers between devices, local(): gram_one = lax.psum(lax.psum(block_gram, 'slab'), 'grp')  151 us
    psum x1, waiting for transfers between devices, local(): gram_two = lax.psum(block_second, ('grp', 'slab'))  133 us
    another operation x12, other arithmetic, orthonormal(): lower_small = jnp.linalg.cholesky(cross)  37.9 us
    another operation x8, other arithmetic, orthonormal(): lax.linalg.triangular_solve(lower_small, widened, left_side=False, lower=...  32 us
    all_to_all x1, blocking collectives, local(): lax.all_to_all(reduced, 'grp', split_axis=1, concat_axis=0, tiled=True)  20.9 us
    dot_general x1, matrix products, local(): block_gram = jnp.einsum('jmi,jmk->ik', tensor, tensor, precision=HIGH)  18.1 us
    dot_general x1, matrix products, local(): reduced = jnp.einsum('jmi,ia->jma', tensor, basis_one, precision=HIGH)  17.6 us
    dot_general x4, matrix products, iterate_basis(): current = orthonormal(jnp.dot(gram, current, precision=HIGH))  11.3 us
  transfers between devices with their start and end apart: 3, of which 3 were waited for; matrix products, arithmetic and copies ran while one was open for 0% of the time, Pallas kernels for 0%

profile of v1, /device:TPU:0, one launch (start us, length us, event | category | flops | bytes accessed | tf_op | source)
XLA Modules:
  0.0 453.9 jit_solution(18090042723905139410)
XLA Ops:
  7.2 18.1 %fusion.4 = f32[672,672]{1,0:T(8,128)} fusion(f32[168,8,672]{2,1,0:T(8,128)} %param.6), kind=kOutput, calls=%fused_computation.5 | convolution fusion | flops 7283146752 | bytes 5419008 | tf_op jit(solution)/shard_map/jmi,jmk->ik/dot_general | solution.py:26
  25.4 64.5 %all-reduce.4.cloned.1.call-done = f32[672,672]{1,0:T(8,128)} async-done(((f32[672,672]{1,0:T(8,128)}), f32[672,672]{1,0:T(8,128)}) %all-reduce.4.cloned.1.call-update) | async-done | bytes 1806352 | tf_op jit(solution)/shard_map/psum | solution.py:27
  90.3 86.2 %all-reduce.6.cloned.1.call-done = f32[672,672]{1,0:T(8,128)} async-done(((f32[672,672]{1,0:T(8,128)}), f32[672,672]{1,0:T(8,128)}) %all-reduce.6.cloned.1.call-update) | async-done | bytes 1806352 | tf_op jit(solution)/shard_map/psum | solution.py:27
  176.6 3.7 fusion.29
  180.8 8.8 %cholesky.74 = f32[96,96]{1,0:T(8,128)S(1)} custom-call(f32[96,96]{1,0:T(8,128)S(1)} %fusion.26), custom_call_target="Cholesky" | custom-call | tf_op jit(solution)/shard_map/jit(cholesky)/cholesky | solution.py:12
  190.2 0.7 fusion.13
  190.9 7.4 %custom-call.8 = f32[1,96,96]{1,2,0:T(8,128)S(1)} custom-call(f32[1,96,96]{2,1,0:T(8,128)S(1)} %fusion.13), custom_call_target="InvertDiagBlocksLowerTriangular" | custom-call | tf_op jit(solution)/shard_map/triangular_solve/custom-call.0 | solution.py:13
  198.7 2.0 fusion.31
  201.2 8.8 %cholesky.85 = f32[96,96]{1,0:T(8,128)S(1)} custom-call(f32[96,96]{1,0:T(8,128)S(1)} %fusion.24), custom_call_target="Cholesky" | custom-call | tf_op jit(solution)/shard_map/jit(cholesky)/cholesky | solution.py:12
  210.6 0.7 fusion.14
  211.3 7.4 %custom-call.9 = f32[1,96,96]{1,2,0:T(8,128)S(1)} custom-call(f32[1,96,96]{2,1,0:T(8,128)S(1)} %fusion.14), custom_call_target="InvertDiagBlocksLowerTriangular" | custom-call | tf_op jit(solution)/shard_map/triangular_solve/custom-call.0 | solution.py:13
  219.1 17.6 %fusion.7 = f32[168,8,96]{2,0,1:T(8,128)S(1)} fusion(f32[168,8,672]{2,1,0:T(8,128)} %param.6, f32[96,672]{1,0:T(8,128)S(1)} %fusion.22), kind=kOutput, calls=%fused_computation.6 | convolution fusion | flops 1040449536 | bytes 4386816 | tf_op jit(solution)/shard_map/jmi,ia->jma/dot_general | solution.py:29
  236.8 20.9 %all_to_all.36 = f32[168,8,96]{2,0,1:T(8,128)S(1)} all-to-all(f32[168,8,96]{2,0,1:T(8,128)S(1)} %fusion.7), channel_id=1, replica_groups=mesh['grp'=4,'slab'=8] {'grp'}, dimensions={1} | all-to-all | bytes 1032192 | tf_op jit(solution)/shard_map/all_to_all | solution.py:30
  257.7 3.1 convolution_bitcast_fusion
  260.8 133.2 %all-reduce.8.cloned.1.call-done = f32[672,672]{1,0:T(8,128)} async-done(((f32[672,672]{1,0:T(8,128)}), f32[672,672]{1,0:T(8,128)}) %all-reduce.8.cloned.1.call-update) | async-done | bytes 1806352 | tf_op jit(solution)/shard_map/psum | solution.py:32
  394.0 3.7 fusion.33
  398.2 8.8 %cholesky.96 = f32[96,96]{1,0:T(8,128)S(1)} custom-call(f32[96,96]{1,0:T(8,128)S(1)} %fusion.21), custom_call_target="Cholesky" | custom-call | tf_op jit(solution)/shard_map/jit(cholesky)/cholesky | solution.py:12
  407.6 0.7 fusion.15
  408.3 7.4 %custom-call.10 = f32[1,96,96]{1,2,0:T(8,128)S(1)} custom-call(f32[1,96,96]{2,1,0:T(8,128)S(1)} %fusion.15), custom_call_target="InvertDiagBlocksLowerTriangular" | custom-call | tf_op jit(solution)/shard_map/triangular_solve/custom-call.0 | solution.py:13
  416.1 2.0 fusion.35
  418.6 8.9 %cholesky.107 = f32[96,96]{1,0:T(8,128)S(1)} custom-call(f32[96,96]{1,0:T(8,128)S(1)} %fusion.19), custom_call_target="Cholesky" | custom-call | tf_op jit(solution)/shard_map/jit(cholesky)/cholesky | solution.py:12
  428.8 7.4 %custom-call.11 = f32[1,96,96]{1,2,0:T(8,128)S(1)} custom-call(f32[1,96,96]{2,1,0:T(8,128)S(1)} %fusion.16), custom_call_target="InvertDiagBlocksLowerTriangular" | custom-call | tf_op jit(solution)/shard_map/triangular_solve/custom-call.0 | solution.py:13
  437.2 9.2 %all_to_all.37 = f32[96,2,96]{2,1,0:T(2,128)S(1)} all-to-all(f32[96,2,96]{2,1,0:T(2,128)S(1)} %copy.38), channel_id=1, replica_groups=mesh['grp'=4,'slab'=8] {'grp'}, dimensions={0} | all-to-all | bytes 147456 | tf_op jit(solution)/shard_map/all_to_all | solution.py:35
  446.5 0.7 copy.39
  (44 shorter events, 8.3 us)
Async XLA Ops:
  7.2 169.4 %copy-start = (f32[672,96]{0,1:T(8,128)S(1)}, f32[672,96]{0,1:T(8,128)}, u32[]{:S(2)}) copy-start(f32[672,96]{0,1:T(8,128)} %param.7) | copy-start | bytes 774148
  7.2 82.7 %all-reduce.4.cloned.1.call-start = ((), (), s32[]{:S(2)}) async-start(), calls=%async_computation.2 | async-start | bytes 4128768 | tf_op jit(solution)/shard_map/psum | solution.py:27
  25.3 151.2 %all-reduce.6.cloned.1.call-start = ((), (), s32[]{:S(2)}) async-start(), calls=%async_computation.3 | async-start | bytes 4128768 | tf_op jit(solution)/shard_map/psum | solution.py:27
  89.9 304.1 %all-reduce.8.cloned.1.call-start = ((), (), s32[]{:S(2)}) async-start(), calls=%async_computation.4 | async-start | bytes 4128768 | tf_op jit(solution)/shard_map/psum | solution.py:32
  176.6 22.1 %copy-start.1 = (f32[672,672]{1,0:T(8,128)S(1)}, f32[672,672]{1,0:T(8,128)}, u32[]{:S(2)}) copy-start(f32[672,672]{1,0:T(8,128)} %all-reduce.6.cloned.1.call-done) | copy-start | bytes 5419012
  219.1 17.7 %copy-start.3 = (f32[96,672]{1,0:T(8,128)}, f32[96,672]{1,0:T(8,128)S(1)}, u32[]{:S(2)}) copy-start(f32[96,672]{1,0:T(8,128)S(1)} %fusion.22) | copy-start | bytes 774148
  394.0 22.1 %copy-start.2 = (f32[672,672]{1,0:T(8,128)S(1)}, f32[672,672]{1,0:T(8,128)}, u32[]{:S(2)}) copy-start(f32[672,672]{1,0:T(8,128)} %all-reduce.8.cloned.1.call-done) | copy-start | bytes 5419012
  436.6 10.5 %copy-start.4 = (f32[96,672]{1,0:T(8,128)}, f32[96,672]{1,0:T(8,128)S(1)}, u32[]{:S(2)}) copy-start(f32[96,672]{1,0:T(8,128)S(1)} %fusion.17) | copy-start | bytes 774148
Sparse Core Ops, SparseCore 0:
  25.4 64.3 all-reduce.3
  92.3 84.2 all-reduce.5
  260.9 133.0 all-reduce.7
